TPU v7x, 32 devices: a whole 2x2x4 slice. The times are simulated.
32 devices in a mesh: gx: 2 (over y), gy: 4 (over x, core), gz: 4 (over z).
Axes of the slice: x: 2, y: 2, z: 4, core: 2. Of those that a mesh axis runs over, the one named last changes fastest.
Arguments:
- probe_bits: int32 [8, 32, 512], P('gx', 'gz', 'gy'), may hold values from -2147483648 to 2147483646
- disorder_levels: int32 [8, 32, 512], P('gx', 'gz', 'gy'), may hold values from -2147483648 to 2147483647, as said below
Outputs:
- moments: float32 [3, 8], replicated
- previous: float32 [8, 8, 128, 512], P(None, 'gx', 'gz', 'gy')
- current: float32 [8, 8, 128, 512], P(None, 'gx', 'gz', 'gy')
Inputs may be any that keep to these rules, and one draw needn't show every extreme that they name: `disorder_levels`: every byte of a word is a level 0 to 255.
All inputs are finite; a program needn't handle non-finite values.
Results may differ from a plain program's by a relative error of at most 0.00002.
Values sent between devices are 32-bit elements; how exact they have to be, the bound alone decides.
A program may use at most 64 MiB of HBM per device.

v0:
```python
import jax
import jax.numpy as jnp
from jax import lax
from jax.sharding import PartitionSpec as P

PROBES = 8
LEVELS = 256


disorder_width = 4.0
spectral_scale = 8.4


def with_halo(cells, sides, width):
    for axis, dim in sides:
        count = lax.axis_size(axis)
        head = lax.slice_in_dim(cells, 0, width, axis=dim)
        tail = lax.slice_in_dim(cells, cells.shape[dim] - width, cells.shape[dim], axis=dim)
        cells = jnp.concatenate(
            [
                lax.ppermute(tail, axis, [(i, (i + 1) % count) for i in range(count)]),
                cells,
                lax.ppermute(head, axis, [((i + 1) % count, i) for i in range(count)]),
            ],
            axis=dim,
        )
    return cells


def unpack_signs(packed):
    shifts = (
        4 * jnp.arange(PROBES, dtype=jnp.int32)[:, None] + jnp.arange(4, dtype=jnp.int32)[None, :]
    )
    bit_values = jnp.right_shift(packed[None, :, :, None, :], shifts[:, None, None, :, None]) & 1
    layout = bit_values.shape
    flat = bit_values.reshape(layout[0], layout[1], layout[2] * layout[3], layout[4])
    return 2.0 * flat.astype(jnp.float32) - 1.0


def unpack_energy(packed):
    shifts = 8 * jnp.arange(4, dtype=jnp.int32)
    levels = jnp.right_shift(packed[:, :, None, :], shifts[None, None, :, None]) & 255
    layout = levels.shape
    flat = levels.reshape(layout[0], layout[1] * layout[2], layout[3])
    return disorder_width * ((flat.astype(jnp.float32) + 0.5) / LEVELS - 0.5)


def crop_sites(block, margin):
    return block[..., margin:-margin, margin:-margin, margin:-margin]


def crop_depth(block, margin):
    return block[..., margin:-margin, :]


def valid_ham(padded, energy):
    center = padded[:, 1:-1, 1:-1, 1:-1]
    beside = padded[:, 2:, 1:-1, 1:-1] + padded[:, :-2, 1:-1, 1:-1]
    beside = beside + padded[:, 1:-1, 1:-1, 2:] + padded[:, 1:-1, 1:-1, :-2]
    beside = beside + padded[:, 1:-1, 2:, 1:-1] + padded[:, 1:-1, :-2, 1:-1]
    return (energy[None] * center - beside) / spectral_scale


def per_device(probe_bits, disorder_levels):
    stacked = jnp.stack([probe_bits, disorder_levels], 0)
    extended = with_halo(stacked, (("gx", 1), ("gy", 3), ("gz", 2)), 3)
    signs_wide = crop_depth(unpack_signs(extended[0]), 9)
    energy_wide = crop_depth(unpack_energy(extended[1]), 9)
    first_wide = valid_ham(signs_wide, crop_sites(energy_wide, 1))
    second_wide = 2.0 * valid_ham(first_wide, crop_sites(energy_wide, 2)) - crop_sites(
        signs_wide, 2
    )
    third = 2.0 * valid_ham(second_wide, crop_sites(energy_wide, 3)) - crop_sites(first_wide, 2)
    signs = crop_sites(signs_wide, 3)
    first = crop_sites(first_wide, 2)
    second = crop_sites(second_wide, 1)
    partial_sums = [jnp.sum(signs * vec, axis=(1, 2, 3)) for vec in (first, second, third)]
    total_sites = (
        third.shape[1]
        * third.shape[2]
        * third.shape[3]
        * lax.axis_size("gx")
        * lax.axis_size("gy")
        * lax.axis_size("gz")
    )
    summed = [lax.psum(part_sum, ("gx", "gy", "gz")) for part_sum in partial_sums]
    moments = jnp.stack(summed) / total_sites
    return (moments, second, third)


def solution(mesh):
    placed = (P("gx", "gz", "gy"), P("gx", "gz", "gy"))
    return jax.shard_map(
        per_device,
        mesh=mesh,
        in_specs=placed,
        out_specs=(P(), P(None, "gx", "gz", "gy"), P(None, "gx", "gz", "gy")),
        check_vma=False,
    )
```

profile of v0, /device:TPU:0, one launch (start us, length us, event | category | flops | bytes accessed | tf_op | source)
XLA Modules:
  0.0 74.9 jit_solution(8602768216348819966)
XLA Ops:
  0.6 0.8 %fusion.7 = (s32[2,3,8,128]{3,2,1,0:T(8,128)S(1)}, s32[2,3,8,128]{3,2,1,0:T(8,128)S(1)}) fusion(s32[1,4,8,128]{3,2,1,0:T(8,128)} %bitcast.10, s32[1,4,8,128]{3,2,1,0:T(8,128)} %bitcast.14), kind=kLoop, calls=%fused_computation.37 | loop fusion | flops 12288 | bytes 81920 | tf_op jit(solution)/shard_map/stack | solution.py:65
  1.4 3.0 %collective-permute-start = (s32[2,3,8,128]{3,2,1,0:T(8,128)S(1)}, s32[2,3,8,128]{3,2,1,0:T(8,128)S(1)}, u32[]{:S(2)}, u32[]{:S(2)}) collective-permute-start(s32[2,3,8,128]{3,2,1,0:T(8,128)S(1)} %get-tuple-element.17), channel_id=1, source_target_pairs={{0,16},{16,0},{1,17},{17,1},{2,18},{18,2},{3,19},{19,3},{4,20},{20... | collective-permute-start | bytes 73736 | tf_op jit(solution)/shard_map/ppermute | solution.py:21
  4.5 1.7 %collective-permute-done = s32[2,3,8,128]{3,2,1,0:T(8,128)S(1)} collective-permute-done((s32[2,3,8,128]{3,2,1,0:T(8,128)S(1)}, s32[2,3,8,128]{3,2,1,0:T(8,128)S(1)}, u32[]{:S(2)}, u32[]{:S(2)}) %collective-permute-start) | collective-permute-done | bytes 24608 | tf_op jit(solution)/shard_map/ppermute | solution.py:21
  6.2 2.0 %collective-permute-done.1 = s32[2,3,8,128]{3,2,1,0:T(8,128)S(1)} collective-permute-done((s32[2,3,8,128]{3,2,1,0:T(8,128)S(1)}, s32[2,3,8,128]{3,2,1,0:T(8,128)S(1)}, u32[]{:S(2)}, u32[]{:S(2)}) %collective-permute-start.1) | collective-permute-done | bytes 24608 | tf_op jit(solution)/shard_map/ppermute | solution.py:23
  8.2 0.7 pad_add_fusion.2
  9.1 1.7 %collective-permute-start.3 = (s32[2,10,8,3]{3,2,1,0:T(8,128)S(1)}, s32[2,10,8,3]{3,2,1,0:T(8,128)S(1)}, u32[]{:S(2)}, u32[]{:S(2)}) collective-permute-start(s32[2,10,8,3]{3,2,1,0:T(8,128)S(1)} %get-tuple-element.16), channel_id=1, source_target_pairs={{4,0},{8,4},{12,8},{0,12},{5,1},{9,5},{13,9},{1,13},{6,2},{10,6},{... | collective-permute-start | bytes 5768 | tf_op jit(solution)/shard_map/ppermute | solution.py:23
  10.9 2.1 %collective-permute-done.2 = s32[2,10,8,3]{3,2,1,0:T(8,128)S(1)} collective-permute-done((s32[2,10,8,3]{3,2,1,0:T(8,128)S(1)}, s32[2,10,8,3]{3,2,1,0:T(8,128)S(1)}, u32[]{:S(2)}, u32[]{:S(2)}) %collective-permute-start.2) | collective-permute-done | bytes 1952 | tf_op jit(solution)/shard_map/ppermute | solution.py:21
  13.0 0.9 %pad_add_fusion.1 = s32[2,10,8,134]{3,2,1,0:T(8,128)S(1)} fusion(s32[2,10,8,3]{3,2,1,0:T(8,128)S(1)} %collective-permute-done.3, s32[2,3,8,128]{3,2,1,0:T(8,128)S(1)} %collective-permute-done.1, s32[1,4,8,128]{3,2,1,0:T(8,128)} %bitcast.16, s32[1,4,8,128]{3,2,1,0:T(8,128)} %bitcast.12, s32[2,3,8,128]{3,2,1,0:T(8,128)S(1)} %collective-permute-done, ...), kind=kLoop, calls=%fused_computation.33 | loop fusion | flops 107200 | bytes 171520 | tf_op jit(solution)/shard_map/concatenate | solution.py:19
  13.9 1.6 %collective-permute-start.4 = (s32[2,10,3,134]{3,2,1,0:T(4,128)S(1)}, s32[2,10,3,134]{3,2,1,0:T(4,128)S(1)}, u32[]{:S(2)}, u32[]{:S(2)}) collective-permute-start(s32[2,10,3,134]{3,2,1,0:T(4,128)S(1)} %get-tuple-element.13), channel_id=1, source_target_pairs={{0,1},{1,2},{2,3},{3,0},{4,5},{5,6},{6,7},{7,4},{8,9},{9,10},{10,1... | collective-permute-start | bytes 96488 | tf_op jit(solution)/shard_map/ppermute | solution.py:21
  15.5 2.2 %collective-permute-start.5 = (s32[2,10,3,134]{3,2,1,0:T(4,128)S(1)}, s32[2,10,3,134]{3,2,1,0:T(4,128)S(1)}, u32[]{:S(2)}, u32[]{:S(2)}) collective-permute-start(s32[2,10,3,134]{3,2,1,0:T(4,128)S(1)} %get-tuple-element.14), channel_id=1, source_target_pairs={{1,0},{2,1},{3,2},{0,3},{5,4},{6,5},{7,6},{4,7},{9,8},{10,9},{11,1... | collective-permute-start | bytes 96488 | tf_op jit(solution)/shard_map/ppermute | solution.py:23
  17.9 2.5 %collective-permute-done.4 = s32[2,10,3,134]{3,2,1,0:T(4,128)S(1)} collective-permute-done((s32[2,10,3,134]{3,2,1,0:T(4,128)S(1)}, s32[2,10,3,134]{3,2,1,0:T(4,128)S(1)}, u32[]{:S(2)}, u32[]{:S(2)}) %collective-permute-start.4) | collective-permute-done | bytes 32192 | tf_op jit(solution)/shard_map/ppermute | solution.py:21
  20.5 1.8 %collective-permute-done.5 = s32[2,10,3,134]{3,2,1,0:T(4,128)S(1)} collective-permute-done((s32[2,10,3,134]{3,2,1,0:T(4,128)S(1)}, s32[2,10,3,134]{3,2,1,0:T(4,128)S(1)}, u32[]{:S(2)}, u32[]{:S(2)}) %collective-permute-start.5) | collective-permute-done | bytes 32192 | tf_op jit(solution)/shard_map/ppermute | solution.py:23
  22.3 0.9 %pad_add_fusion = s32[2,10,14,134]{3,2,1,0:T(8,128)S(1)} fusion(s32[2,10,3,134]{3,2,1,0:T(4,128)S(1)} %collective-permute-done.5, s32[2,10,8,3]{3,2,1,0:T(8,128)S(1)} %collective-permute-done.3, s32[2,3,8,128]{3,2,1,0:T(8,128)S(1)} %collective-permute-done.1, s32[1,4,8,128]{3,2,1,0:T(8,128)} %bitcast.17, s32[1,4,8,128]{3,2,1,0:T(8,128)} %bitcast.13, ...), kind=kLoop, calls=%fused_computation.30 | loop fusion | flops 262640 | bytes 300160 | tf_op jit(solution)/shard_map/concatenate | solution.py:19
  23.4 0.2 shift_right_arithmetic.56
  23.6 0.2 add_multiply_fusion
  23.9 0.1 slice.174
  24.0 0.2 slice.165
  24.3 0.2 shift_right_arithmetic.48
  24.5 0.8 %multiply_add_fusion = f32[8,10,56,134]{3,2,1,0:T(8,128)S(1)} fusion(s32[8,56]{1,0:T(8,128)S(1)} %copy.5, s32[10,56,134]{2,1,0:T(8,128)S(1)} %shift_right_arithmetic.48), kind=kLoop, calls=%fused_computation | loop fusion | flops 3001600 | bytes 2703232 | tf_op jit(solution)/shard_map/sub | solution.py:37
  25.3 4.5 %fusion.1 = f32[8,8,36,132]{3,2,1,0:T(8,128)S(1)} fusion(f32[8,10,56,134]{3,2,1,0:T(8,128)S(1)} %multiply_add_fusion, f32[8,36,132]{2,1,0:T(8,128)S(1)} %slice.165), kind=kLoop, calls=%fused_computation.3 | loop fusion | flops 2433024 | bytes 9884160 | tf_op jit(solution)/shard_map/div | solution.py:61
  29.8 3.6 %slice_subtract_fusion = f32[8,6,34,130]{3,2,1,0:T(8,128)S(1)} fusion(f32[8,10,56,134]{3,2,1,0:T(8,128)S(1)} %multiply_add_fusion, f32[8,8,36,132]{3,2,1,0:T(8,128)S(1)} %fusion.1, f32[6,34,130]{2,1,0:T(8,128)S(1)} %slice.174), kind=kLoop, calls=%fused_computation.9 | loop fusion | flops 1909440 | bytes 7743840 | tf_op jit(solution)/shard_map/sub | solution.py:70
  33.5 2.1 %multiply_reduce_fusion.2 = (f32[8]{0:T(128)S(1)}, f32[8]{0:T(128)S(1)}, f32[8]{0:T(128)S(1)}, f32[8,4,32,128]{3,2,1,0:T(8,128)}, f32[8,4,32,128]{3,2,1,0:T(8,128)}) fusion(f32[8,8,36,132]{3,2,1,0:T(8,128)S(1)} %fusion.1, f32[8,10,56,134]{3,2,1,0:T(8,128)S(1)} %multiply_add_fusion, f32[8,6,34,130]{3,2,1,0:T(8,128)S(1)} %slice_subtract_fusion, ...), kind=kLoop, calls=%fused_computation.29 | loop fusion | flops 1966056 | bytes 5832800 | tf_op jit(solution)/shard_map/reduce_sum | solution.py:77
  35.6 38.7 %all-reduce = (f32[1,8]{1,0:T(1,128)S(1)}, f32[1,8]{1,0:T(1,128)S(1)}, f32[1,8]{1,0:T(1,128)S(1)}) all-reduce(f32[1,8]{1,0:T(1,128)S(1)} %bitcast.21, f32[1,8]{1,0:T(1,128)S(1)} %bitcast.20, f32[1,8]{1,0:T(1,128)S(1)} %bitcast.19), channel_id=1, replica_groups=mesh['gx'=2,'gy'=4,'gz'=4] {'gx','gy','gz'}, use_global_device_ids=true, to_apply=%region_5.0 | all-reduce | flops 24 | bytes 192 | tf_op jit(solution)/shard_map/psum | solution.py:86
  74.3 0.6 maximum_multiply_fusion
  (16 shorter events, 0.7 us)
Async XLA Ops:
  1.4 4.8 %collective-permute-start = (s32[2,3,8,128]{3,2,1,0:T(8,128)S(1)}, s32[2,3,8,128]{3,2,1,0:T(8,128)S(1)}, u32[]{:S(2)}, u32[]{:S(2)}) collective-permute-start(s32[2,3,8,128]{3,2,1,0:T(8,128)S(1)} %get-tuple-element.17), channel_id=1, source_target_pairs={{0,16},{16,0},{1,17},{17,1},{2,18},{18,2},{3,19},{19,3},{4,20},{20... | collective-permute-start | bytes 73736 | tf_op jit(solution)/shard_map/ppermute | solution.py:21
  4.4 3.8 %collective-permute-start.1 = (s32[2,3,8,128]{3,2,1,0:T(8,128)S(1)}, s32[2,3,8,128]{3,2,1,0:T(8,128)S(1)}, u32[]{:S(2)}, u32[]{:S(2)}) collective-permute-start(s32[2,3,8,128]{3,2,1,0:T(8,128)S(1)} %get-tuple-element.18), channel_id=1, source_target_pairs={{16,0},{0,16},{17,1},{1,17},{18,2},{2,18},{19,3},{3,19},{20,4},{4,... | collective-permute-start | bytes 73736 | tf_op jit(solution)/shard_map/ppermute | solution.py:23
  9.1 3.9 %collective-permute-start.2 = (s32[2,10,8,3]{3,2,1,0:T(8,128)S(1)}, s32[2,10,8,3]{3,2,1,0:T(8,128)S(1)}, u32[]{:S(2)}, u32[]{:S(2)}) collective-permute-start(s32[2,10,8,3]{3,2,1,0:T(8,128)S(1)} %get-tuple-element.15), channel_id=1, source_target_pairs={{0,4},{4,8},{8,12},{12,0},{1,5},{5,9},{9,13},{13,1},{2,6},{6,10},{... | collective-permute-start | bytes 5768 | tf_op jit(solution)/shard_map/ppermute | solution.py:21
  9.1 3.9 %collective-permute-start.3 = (s32[2,10,8,3]{3,2,1,0:T(8,128)S(1)}, s32[2,10,8,3]{3,2,1,0:T(8,128)S(1)}, u32[]{:S(2)}, u32[]{:S(2)}) collective-permute-start(s32[2,10,8,3]{3,2,1,0:T(8,128)S(1)} %get-tuple-element.16), channel_id=1, source_target_pairs={{4,0},{8,4},{12,8},{0,12},{5,1},{9,5},{13,9},{1,13},{6,2},{10,6},{... | collective-permute-start | bytes 5768 | tf_op jit(solution)/shard_map/ppermute | solution.py:23
  13.9 6.6 %collective-permute-start.4 = (s32[2,10,3,134]{3,2,1,0:T(4,128)S(1)}, s32[2,10,3,134]{3,2,1,0:T(4,128)S(1)}, u32[]{:S(2)}, u32[]{:S(2)}) collective-permute-start(s32[2,10,3,134]{3,2,1,0:T(4,128)S(1)} %get-tuple-element.13), channel_id=1, source_target_pairs={{0,1},{1,2},{2,3},{3,0},{4,5},{5,6},{6,7},{7,4},{8,9},{9,10},{10,1... | collective-permute-start | bytes 96488 | tf_op jit(solution)/shard_map/ppermute | solution.py:21
  15.5 6.8 %collective-permute-start.5 = (s32[2,10,3,134]{3,2,1,0:T(4,128)S(1)}, s32[2,10,3,134]{3,2,1,0:T(4,128)S(1)}, u32[]{:S(2)}, u32[]{:S(2)}) collective-permute-start(s32[2,10,3,134]{3,2,1,0:T(4,128)S(1)} %get-tuple-element.14), channel_id=1, source_target_pairs={{1,0},{2,1},{3,2},{0,3},{5,4},{6,5},{7,6},{4,7},{9,8},{10,9},{11,1... | collective-permute-start | bytes 96488 | tf_op jit(solution)/shard_map/ppermute | solution.py:23
where the time goes:
time: 75.8 us; the launch traced here: 74.9 us
  blocking collectives  38.7 us (51%)
  other arithmetic  15.2 us (20%)
  waiting for transfers between devices  10.2 us (13%)
  starting transfers between devices  8.74 us (12%)
  local copies, waits for them, and re-layouts  1.25 us (2%)
  between operations  0.76 us (1%)
    psum x1, blocking collectives, per_device(): lax.psum(part_sum, ('gx', 'gy', 'gz'))  38.7 us
    ppermute x3, waiting for transfers between devices, with_halo(): lax.ppermute(tail, axis, [(i, (i + 1) % count) for i in range(count)])  6.36 us
    ppermute x3, starting transfers between devices, with_halo(): lax.ppermute(tail, axis, [(i, (i + 1) % count) for i in range(count)])  4.68 us
    div x1, other arithmetic, valid_ham(): return (energy[None] * center - beside) / spectral_scale  4.54 us
    ppermute x3, starting transfers between devices, with_halo(): lax.ppermute(head, axis, [((i + 1) % count, i) for i in range(count)])  4.05 us
    ppermute x3, waiting for transfers between devices, with_halo(): lax.ppermute(head, axis, [((i + 1) % count, i) for i in range(count)])  3.84 us
    sub x1, other arithmetic, per_device(): 2.0 * valid_ham(first_wide, crop_sites(energy_wide, 2))  3.64 us
    concatenate x3, other arithmetic, with_halo(): jnp.concatenate([lax.ppermute(tail, axis, [(i, (i + 1) % count) for i in...  2.53 us
  transfers between devices with their start and end apart: 6, of which 5 were waited for; matrix products, arithmetic and copies ran while one was open for 0% of the time, Pallas kernels for 0%

commit v1 on v0

v1 whole, which is shorter than its diff:
```python
import functools

import jax
import jax.numpy as jnp
from jax import lax
from jax.experimental import pallas as pl
from jax.experimental.pallas import tpu as pltpu
from jax.sharding import PartitionSpec as P

PROBES = 8
LEVELS = 256
LANES = 128
SITES = 4
STRIP = 12

disorder_width = 4.0
spectral_scale = 8.4
MESH = pl.DeviceIdType.MESH


def kernel(names, sizes, p_ref, d_ref, prow_ref, drow_ref, mom_ref, prev_ref, cur_ref,
           words, packs, strips, v0, v1, v2, en, s0, s1, s2, se, moms,
           send_sem, recv_sem, msend_sem, mrecv_sem):
    X, W, _ = p_ref.shape
    Z = SITES * W
    nbx = packs.shape[0]
    M = nbx * X
    gx, gy, gz = sizes["gx"], sizes["gy"], sizes["gz"]
    ix, iy, iz = (lax.axis_index(a) for a in ("gx", "gy", "gz"))
    total = gx * gy * gz
    me = (ix * gy + iy) * gz + iz

    def device(x, y, z):
        at = {"gx": x, "gy": y, "gz": z}
        return tuple(at[a] for a in names)

    def nth(k):
        t = lax.rem(me + k, total)
        return device(t // (gy * gz), lax.rem(t // gz, gy), lax.rem(t, gz)), t

    barrier = pltpu.get_barrier_semaphore()

    def greet(k, _):
        pl.semaphore_signal(barrier, inc=1, device_id=nth(k)[0], device_id_type=MESH)
        return 0

    lax.fori_loop(1, total, greet, 0)

    lane = lax.broadcasted_iota(jnp.int32, (2 * X, LANES), 1)
    slot_word = (lane * 10923) >> 17
    column = lane - STRIP * slot_word

    pack = jnp.zeros((2 * X, LANES), jnp.int32)
    for w in range(W):
        rows = jnp.concatenate([p_ref[:, w, :], d_ref[:, w, :]], axis=0)
        base = STRIP * (w + 1)
        first = pltpu.roll(rows, (base - (LANES - 3)) % LANES, 1)
        second = pltpu.roll(rows, (base + 5 - (LANES - 2)) % LANES, 1)
        pack = jnp.where(slot_word == w + 1, jnp.where(column < 5, first, second), pack)
    packs[0, 1, 1] = pack
    for f, ref in enumerate((prow_ref, drow_ref)):
        words[f, 0:X, 1:W + 1] = ref[...]

    pl.semaphore_wait(barrier, total - 1)

    xs = (0, 1) if nbx == 2 else (0, 1, -1)
    slot_of = {0: 0, 1: nbx - 1, -1: 1}
    copies = []
    for ox in xs:
        for oz in (0, 1, -1):
            for oy in (0, 1, -1):
                if ox == 0 and oz == 0 and oy == 0:
                    continue
                to = device(lax.rem(ix + ox + gx, gx), lax.rem(iy + oy + gy, gy), lax.rem(iz + oz + gz, gz))
                s = slot_of[ox]
                moves = []
                if oy == 0:
                    src_w, dst_w = {0: (pl.ds(0, W), pl.ds(1, W)), 1: (pl.ds(W - 1, 1), pl.ds(0, 1)),
                                    -1: (pl.ds(0, 1), pl.ds(W + 1, 1))}[oz]
                    for f, ref in enumerate((prow_ref, drow_ref)):
                        moves.append((ref.at[:, src_w], words.at[f, pl.ds(s * X, X), dst_w]))
                moves.append((packs.at[0, 1, 1], packs.at[s, 1 - oz, 1 - oy]))
                for src, dst in moves:
                    n = len(copies)
                    copies.append(pltpu.make_async_remote_copy(
                        src_ref=src, dst_ref=dst, send_sem=send_sem.at[n], recv_sem=recv_sem.at[n],
                        device_id=to, device_id_type=MESH))
    for copy in copies:
        copy.start()
    for copy in copies:
        copy.wait()

    scale = 1.0 / spectral_scale
    e_mul = disorder_width / LEVELS / spectral_scale
    e_add = disorder_width * (0.5 / LEVELS - 0.5) / spectral_scale
    probe = lax.broadcasted_iota(jnp.int32, (PROBES, LANES), 0)
    lane8 = lax.broadcasted_iota(jnp.int32, (PROBES, LANES), 1)
    col8 = lane8 - STRIP * ((lane8 * 10923) >> 17)
    lifts = [31 - (SITES * probe + j) for j in range(SITES)]

    def sign_of(row, j):
        return jnp.where((jnp.broadcast_to(row, (PROBES, LANES)) << lifts[j]) < 0, 1.0, -1.0).astype(jnp.float32)

    def energy_of(row, j):
        level = (jnp.broadcast_to(row, (PROBES, LANES)) >> (8 * j)) & 255
        return level.astype(jnp.float32) * e_mul + e_add

    for s in range(nbx):
        def joined(oz):
            return jnp.where(column < 3, packs[s, oz, 0], jnp.where(column < 7, packs[s, oz, 1], packs[s, oz, 2]))
        strip = jnp.where(slot_word == 0, pltpu.roll(joined(0), (-STRIP * W) % LANES, 1), joined(1))
        strips[s] = jnp.where(slot_word == W + 1, pltpu.roll(joined(2), (STRIP * W) % LANES, 1), strip)
        for x in range(X):
            for j in range(SITES):
                s0[s * X + x, j] = sign_of(strips[s, x:x + 1], j)
                se[s * X + x, j] = energy_of(strips[s, X + x:X + x + 1], j)

    def plane(e):
        return lax.rem(e + M, M)

    def unpack(i, _):
        q = plane(i - 3)
        for z in range(-3, Z + 3):
            w, j = divmod(z + SITES, SITES)
            v0[q, z + 3] = sign_of(words[0, q, w], j)
            en[q, z + 3] = energy_of(words[1, q, w], j)
        return 0

    lax.fori_loop(0, min(M, X + 6), unpack, 0)

    def strip_sum(src, q, up, down):
        mine = [src[q, j] for j in range(SITES)]
        sums = []
        for j in range(SITES):
            z_up = mine[j + 1] if j + 1 < SITES else pltpu.roll(mine[0], LANES - STRIP, 1)
            z_down = mine[j - 1] if j > 0 else pltpu.roll(mine[SITES - 1], STRIP, 1)
            sums.append(src[up, j] + src[down, j] + pltpu.roll(mine[j], LANES - 1, 1)
                        + pltpu.roll(mine[j], 1, 1) + z_up + z_down)
        return mine, sums

    def edges_of(mine):
        return [jnp.where(col8 == 1, pltpu.roll(m, LANES - 6, 1), m) for m in mine]

    def site_sum(src, q, up, down, z, edges):
        w, j = divmod(z + SITES, SITES)
        fix = pltpu.roll(edges[j], (-(STRIP * w + 2)) % LANES, 1)
        mid = src[q, z + 3]
        right = jnp.where(lane8 == LANES - 1, fix, pltpu.roll(mid, LANES - 1, 1))
        left = jnp.where(lane8 == 0, fix, pltpu.roll(mid, 1, 1))
        return mid, src[up, z + 3] + src[down, z + 3] + right + left + src[q, z + 4] + src[q, z + 2]

    zero = jnp.zeros((PROBES, LANES), jnp.float32)

    def first_level(i, accs):
        e = i - 2
        q, up, down = plane(e), plane(e + 1), plane(e + M - 1)
        mine, sums = strip_sum(s0, q, up, down)
        for j in range(SITES):
            s1[q, j] = se[q, j] * mine[j] - scale * sums[j]
        edges = edges_of(mine)
        one, two = zero, zero
        for z in range(-2, Z + 2):
            mid, total_six = site_sum(v0, q, up, down, z, edges)
            new = en[q, z + 3] * mid - scale * total_six
            v1[q, z + 3] = new
            if 0 <= z < Z:
                one, two = one + mid * new, two + new * new
        own = jnp.where((e >= 0) & (e < X), 1.0, 0.0).astype(jnp.float32)
        return accs[0] + own * one, accs[1] + own * two

    m1, m2 = lax.fori_loop(0, min(M, X + 4), first_level, (zero, zero))

    def second_level(i, acc):
        e = i - 1
        q, up, down = plane(e), plane(e + 1), plane(e + M - 1)
        mine, sums = strip_sum(s1, q, up, down)
        for j in range(SITES):
            s2[q, j] = 2.0 * (se[q, j] * mine[j] - scale * sums[j]) - s0[q, j]
        edges = edges_of(mine)
        three = zero
        for z in range(-1, Z + 1):
            mid, total_six = site_sum(v1, q, up, down, z, edges)
            new = 2.0 * (en[q, z + 3] * mid - scale * total_six) - v0[q, z + 3]
            v2[q, z + 3] = new
            if 0 <= z < Z:
                three = three + mid * new
        own = jnp.where((e >= 0) & (e < X), 1.0, 0.0).astype(jnp.float32)
        return acc + own * three

    m3 = lax.fori_loop(0, X + 2, second_level, zero)

    row = zero
    for n, acc in enumerate((m1, m2, m3)):
        summed = jnp.broadcast_to(jnp.sum(acc, axis=1, keepdims=True), (PROBES, LANES))
        row = row + jnp.where(lane8 == PROBES * n + probe, summed, 0.0)
    moms[me] = jnp.sum(row, axis=0, keepdims=True)

    def moment_copy(k):
        to, t = nth(k)
        out = pltpu.make_async_remote_copy(
            src_ref=moms.at[me], dst_ref=moms.at[me], send_sem=msend_sem.at[t], recv_sem=mrecv_sem.at[me],
            device_id=to, device_id_type=MESH)
        back = pltpu.make_async_remote_copy(
            src_ref=moms.at[me], dst_ref=moms.at[t], send_sem=msend_sem.at[t], recv_sem=mrecv_sem.at[t],
            device_id=to, device_id_type=MESH)
        return out, back

    def send(k, _):
        moment_copy(k)[0].start()
        return 0

    lax.fori_loop(1, total, send, 0)

    def third_level(x, _):
        q, up, down = plane(x), plane(x + 1), plane(x + M - 1)
        edges = edges_of([s2[q, j] for j in range(SITES)])
        for z in range(Z):
            mid, total_six = site_sum(v2, q, up, down, z, edges)
            new = 2.0 * (en[q, z + 3] * mid - scale * total_six) - v1[q, z + 3]
            at = pl.ds(x * Z + z, PROBES, stride=X * Z)
            prev_ref[at, :] = mid
            cur_ref[at, :] = new
        return 0

    lax.fori_loop(0, X, third_level, 0)

    def land(k, _):
        out, back = moment_copy(k)
        out.wait_send()
        back.wait_recv()
        return 0

    lax.fori_loop(1, total, land, 0)
    sites = total * X * Z * LANES
    sums = jnp.sum(moms[...], axis=0) * (1.0 / sites)
    first = sums
    second = 2.0 * pltpu.roll(sums, LANES - PROBES, 1) - 1.0
    third = 2.0 * pltpu.roll(sums, LANES - 2 * PROBES, 1) - sums
    mom_ref[...] = jnp.concatenate([first, second, third], axis=0)[:, :PROBES]


def per_device(names, sizes, probe_bits, disorder_levels):
    X, W, Y = probe_bits.shape
    if Y != LANES or STRIP * (W + 2) > LANES or X < 3:
        raise ValueError("block size")
    Z = SITES * W
    nbx = 2 if sizes["gx"] == 2 else 3
    M = nbx * X
    n_copies = (9 * nbx - 1) + 2 * (3 * nbx - 1)
    total = sizes["gx"] * sizes["gy"] * sizes["gz"]
    rows = (X, W, 1, Y)
    vmem = pl.BlockSpec(memory_space=pltpu.VMEM)
    f32, i32 = jnp.float32, jnp.int32
    tile = (PROBES, LANES)
    moments, previous, current = pl.pallas_call(
        functools.partial(kernel, names, sizes),
        out_shape=(
            jax.ShapeDtypeStruct((3, PROBES), f32),
            jax.ShapeDtypeStruct((PROBES * X * Z, Y), f32),
            jax.ShapeDtypeStruct((PROBES * X * Z, Y), f32),
        ),
        in_specs=[vmem] * 4,
        out_specs=(vmem,) * 3,
        scratch_shapes=[
            pltpu.VMEM((2, M, W + 2, 1, LANES), i32),
            pltpu.VMEM((nbx, 3, 3, 2 * X, LANES), i32),
            pltpu.VMEM((nbx, 2 * X, LANES), i32),
            pltpu.VMEM((M, Z + 6) + tile, f32),
            pltpu.VMEM((M, Z + 6) + tile, f32),
            pltpu.VMEM((M, Z + 6) + tile, f32),
            pltpu.VMEM((M, Z + 6) + tile, f32),
            pltpu.VMEM((M, SITES) + tile, f32),
            pltpu.VMEM((M, SITES) + tile, f32),
            pltpu.VMEM((M, SITES) + tile, f32),
            pltpu.VMEM((M, SITES) + tile, f32),
            pltpu.VMEM((total, 1, LANES), f32),
            pltpu.SemaphoreType.DMA((n_copies,)),
            pltpu.SemaphoreType.DMA((n_copies,)),
            pltpu.SemaphoreType.DMA((total,)),
            pltpu.SemaphoreType.DMA((total,)),
        ],
        compiler_params=pltpu.CompilerParams(collective_id=0, has_side_effects=True,
                                             vmem_limit_bytes=40 * 1024 * 1024),
    )(probe_bits, disorder_levels, probe_bits.reshape(rows), disorder_levels.reshape(rows))
    shape = (PROBES, X, Z, Y)
    return moments, previous.reshape(shape), current.reshape(shape)


def solution(mesh):
    placed = (P("gx", "gz", "gy"), P("gx", "gz", "gy"))
    sizes = {a: mesh.shape[a] for a in mesh.axis_names}
    return jax.shard_map(
        functools.partial(per_device, tuple(mesh.axis_names), sizes),
        mesh=mesh,
        in_specs=placed,
        out_specs=(P(), P(None, "gx", "gz", "gy"), P(None, "gx", "gz", "gy")),
        check_vma=False,
    )
```

time: 75.8 us -> 25.6 us (0.34)
  blocking collectives: 38.7 us -> 0 us
  Pallas kernels: 0 us -> 21 us
  other arithmetic: 15.2 us -> 0 us
  waiting for transfers between devices: 10.2 us -> 0 us
  starting transfers between devices: 8.74 us -> 0 us
  local copies, waits for them, and re-layouts: 1.25 us -> 3.59 us
    psum x1 -> x0, blocking collectives: 38.7 us -> none  [per_device(): lax.psum(part_sum, ('gx', 'gy', 'gz'))]
    pallas_call x0 -> x1, Pallas kernels: none -> 21 us  [per_device(): pl.pallas_call(functools.partial(kernel, names, sizes), out_shape=(jax.Sh...]
    ppermute x6 -> x0, waiting for transfers between devices: 10.2 us -> none  [the longest x3 6.36 us: with_halo(): lax.ppermute(tail, axis, [(i, (i + 1) % count) for i in range(count)])]
    ppermute x6 -> x0, starting transfers between devices: 8.74 us -> none  [the longest x3 4.68 us: with_halo(): lax.ppermute(tail, axis, [(i, (i + 1) % count) for i in range(count)])]
    div x2 -> x0, other arithmetic: 5.13 us -> none  [the longest x1 4.54 us: valid_ham(): return (energy[None] * center - beside) / spectral_scale]
    sub x2 -> x0, other arithmetic: 4.44 us -> none  [the longest x1 3.64 us: per_device(): 2.0 * valid_ham(first_wide, crop_sites(energy_wide, 2))]
    unnamed x0 -> x7, local copies, waits for them, and re-layouts: none -> 3.59 us
    concatenate x3 -> x0, other arithmetic: 2.53 us -> none  [with_halo(): jnp.concatenate([lax.ppermute(tail, axis, [(i, (i + 1) % count) for i in...]
  transfers between devices with their start and end apart: 6 -> 0, of which waited for: 5 -> 0; matrix products, arithmetic and copies ran while one was open for 0% -> 0% of each run, Pallas kernels for 0% -> 0%
where the time goes in v1:
time: 25.6 us; the launch traced here: 25.2 us
  Pallas kernels  21 us (82%)
  local copies, waits for them, and re-layouts  3.59 us (14%)
  between operations  0.65 us (3%)
    pallas_call x1, Pallas kernels, per_device(): pl.pallas_call(functools.partial(kernel, names, sizes), out_shape=(jax.Sh...  21 us
    unnamed x7, local copies, waits for them, and re-layouts  3.59 us

profile of v1, /device:TPU:0, one launch (start us, length us, event | category | flops | bytes accessed | tf_op | source)
XLA Modules:
  0.0 25.2 jit_solution(581021369027790653)
XLA Ops:
  0.6 0.0 copy-start
  0.6 0.7 %copy-done = s32[4,8,128]{2,1,0:T(8,128)S(1)} copy-done((s32[4,8,128]{2,1,0:T(8,128)S(1)}, s32[4,8,128]{2,1,0:T(8,128)}, u32[]{:S(2)}) %copy-start) | copy-done | bytes 16408
  1.3 0.0 copy-start.1
  1.4 0.7 %copy-done.1 = s32[4,8,128]{2,1,0:T(8,128)S(1)} copy-done((s32[4,8,128]{2,1,0:T(8,128)S(1)}, s32[4,8,128]{2,1,0:T(8,128)}, u32[]{:S(2)}) %copy-start.1) | copy-done | bytes 16408
  2.1 21.0 %shard_map.49 = (f32[3,8]{1,0:T(4,128)S(1)}, f32[1024,128]{1,0:T(8,128)S(1)}, f32[1024,128]{1,0:T(8,128)S(1)}) custom-call(s32[4,8,128]{2,1,0:T(8,128)S(1)} %copy-done, s32[4,8,128]{2,1,0:T(8,128)S(1)} %copy-done.1, s32[4,8,1,128]{3,2,1,0:T(1,128)S(1)} %bitcast.6, s32[4,8,1,128]{3,2,1,0:T(1,128)S(1)} %bitcast.7), custom_call_target="tpu_custom_call" | custom-call | tf_op jit(solution)/shard_map/pallas_call | solution.py:255
  23.1 0.6 %copy.8 = f32[3,8]{1,0:T(4,128)} copy(f32[3,8]{1,0:T(4,128)S(1)} %get-tuple-element.12) | data formatting | bytes 192
  23.7 0.8 %copy.9 = f32[8,4,32,128]{3,2,1,0:T(8,128)} copy(f32[8,4,32,128]{3,2,1,0:T(8,128)S(1)} %bitcast.5) | data formatting | bytes 1048576
  24.5 0.8 %copy.10 = f32[8,4,32,128]{3,2,1,0:T(8,128)} copy(f32[8,4,32,128]{3,2,1,0:T(8,128)S(1)} %bitcast.4) | data formatting | bytes 1048576
Async XLA Ops:
  0.6 0.7 %copy-start = (s32[4,8,128]{2,1,0:T(8,128)S(1)}, s32[4,8,128]{2,1,0:T(8,128)}, u32[]{:S(2)}) copy-start(s32[4,8,128]{2,1,0:T(8,128)} %p_ref.1) | copy-start | bytes 49156
  1.3 0.7 %copy-start.1 = (s32[4,8,128]{2,1,0:T(8,128)S(1)}, s32[4,8,128]{2,1,0:T(8,128)}, u32[]{:S(2)}) copy-start(s32[4,8,128]{2,1,0:T(8,128)} %d_ref.1) | copy-start | bytes 49156

commit v2 on v1

--- a/solution.py
+++ b/solution.py
@@ -18,9 +18,9 @@
 MESH = pl.DeviceIdType.MESH
 
 
-def kernel(names, sizes, p_ref, d_ref, prow_ref, drow_ref, mom_ref, prev_ref, cur_ref,
-           words, packs, strips, v0, v1, v2, en, s0, s1, s2, se, moms,
-           send_sem, recv_sem, msend_sem, mrecv_sem):
+def kernel(names, sizes, p_hbm, d_hbm, prow_hbm, drow_hbm, mom_ref, prev_ref, cur_ref,
+           p_ref, d_ref, words, packs, strips, v0, v1, v2, en, s0, s1, s2, se, moms,
+           load_sem, send_sem, recv_sem, msend_sem, mrecv_sem):
     X, W, _ = p_ref.shape
     Z = SITES * W
     nbx = packs.shape[0]
@@ -34,22 +34,49 @@
         at = {"gx": x, "gy": y, "gz": z}
         return tuple(at[a] for a in names)
 
-    def nth(k):
-        t = lax.rem(me + k, total)
-        return device(t // (gy * gz), lax.rem(t // gz, gy), lax.rem(t, gz)), t
+    loads = [pltpu.make_async_copy(src, dst, load_sem.at[n]) for n, (src, dst) in enumerate((
+        (p_hbm, p_ref), (d_hbm, d_ref),
+        (prow_hbm, words.at[0, pl.ds(0, X), pl.ds(1, W)]), (drow_hbm, words.at[1, pl.ds(0, X), pl.ds(1, W)])))]
+    for load in loads:
+        load.start()
+
+    def around(at, size):
+        steps = [at]
+        for _ in range(size - 1):
+            steps.append(jnp.where(steps[-1] + 1 == size, 0, steps[-1] + 1))
+        return steps
+
+    around_x, around_y = around(ix, gx), around(iy, gy)
+
+    def each_other(act):
+        for x in range(gx):
+            for y in range(gy):
+                if x or y:
+                    act(device(around_x[x], around_y[y], iz))
+
+        def at_depth(z):
+            for x in range(gx):
+                for y in range(gy):
+                    act(device(around_x[x], around_y[y], z))
+
+        if gz <= 4:
+            for z in around(iz, gz)[1:]:
+                at_depth(z)
+        else:
+            def step(k, _):
+                at_depth(lax.rem(iz + k, gz))
+                return 0
+            lax.fori_loop(1, gz, step, 0)
 
     barrier = pltpu.get_barrier_semaphore()
-
-    def greet(k, _):
-        pl.semaphore_signal(barrier, inc=1, device_id=nth(k)[0], device_id_type=MESH)
-        return 0
-
-    lax.fori_loop(1, total, greet, 0)
+    each_other(lambda to: pl.semaphore_signal(barrier, inc=1, device_id=to, device_id_type=MESH))
 
     lane = lax.broadcasted_iota(jnp.int32, (2 * X, LANES), 1)
     slot_word = (lane * 10923) >> 17
     column = lane - STRIP * slot_word
 
+    for load in loads:
+        load.wait()
     pack = jnp.zeros((2 * X, LANES), jnp.int32)
     for w in range(W):
         rows = jnp.concatenate([p_ref[:, w, :], d_ref[:, w, :]], axis=0)
@@ -58,8 +85,6 @@
         second = pltpu.roll(rows, (base + 5 - (LANES - 2)) % LANES, 1)
         pack = jnp.where(slot_word == w + 1, jnp.where(column < 5, first, second), pack)
     packs[0, 1, 1] = pack
-    for f, ref in enumerate((prow_ref, drow_ref)):
-        words[f, 0:X, 1:W + 1] = ref[...]
 
     pl.semaphore_wait(barrier, total - 1)
 
@@ -75,10 +100,10 @@
                 s = slot_of[ox]
                 moves = []
                 if oy == 0:
-                    src_w, dst_w = {0: (pl.ds(0, W), pl.ds(1, W)), 1: (pl.ds(W - 1, 1), pl.ds(0, 1)),
-                                    -1: (pl.ds(0, 1), pl.ds(W + 1, 1))}[oz]
-                    for f, ref in enumerate((prow_ref, drow_ref)):
-                        moves.append((ref.at[:, src_w], words.at[f, pl.ds(s * X, X), dst_w]))
+                    src_w, dst_w = {0: (pl.ds(1, W), pl.ds(1, W)), 1: (pl.ds(W, 1), pl.ds(0, 1)),
+                                    -1: (pl.ds(1, 1), pl.ds(W + 1, 1))}[oz]
+                    for f in range(2):
+                        moves.append((words.at[f, pl.ds(0, X), src_w], words.at[f, pl.ds(s * X, X), dst_w]))
                 moves.append((packs.at[0, 1, 1], packs.at[s, 1 - oz, 1 - oy]))
                 for src, dst in moves:
                     n = len(copies)
@@ -87,9 +112,6 @@
                         device_id=to, device_id_type=MESH))
     for copy in copies:
         copy.start()
-    for copy in copies:
-        copy.wait()
-
     scale = 1.0 / spectral_scale
     e_mul = disorder_width / LEVELS / spectral_scale
     e_add = disorder_width * (0.5 / LEVELS - 0.5) / spectral_scale
@@ -104,6 +126,20 @@
     def energy_of(row, j):
         level = (jnp.broadcast_to(row, (PROBES, LANES)) >> (8 * j)) & 255
         return level.astype(jnp.float32) * e_mul + e_add
+
+    def unpack(q, zs):
+        for z in zs:
+            w, j = divmod(z + SITES, SITES)
+            v0[q, z + 3] = sign_of(words[0, q, w], j)
+            en[q, z + 3] = energy_of(words[1, q, w], j)
+
+    def unpack_own(x, _):
+        unpack(x, range(Z))
+        return 0
+
+    lax.fori_loop(0, X, unpack_own, 0)
+    for copy in copies:
+        copy.wait()
 
     for s in range(nbx):
         def joined(oz):
@@ -118,15 +154,24 @@
     def plane(e):
         return lax.rem(e + M, M)
 
-    def unpack(i, _):
-        q = plane(i - 3)
-        for z in range(-3, Z + 3):
-            w, j = divmod(z + SITES, SITES)
-            v0[q, z + 3] = sign_of(words[0, q, w], j)
-            en[q, z + 3] = energy_of(words[1, q, w], j)
-        return 0
-
-    lax.fori_loop(0, min(M, X + 6), unpack, 0)
+    def unpack_rim(x, _):
+        unpack(x, [*range(-3, 0), *range(Z, Z + 3)])
+        return 0
+
+    def unpack_far(i, _):
+        unpack(plane(X + i), range(-3, Z + 3))
+        return 0
+
+    def unpack_low(i, _):
+        unpack(plane(i - 3), range(-3, Z + 3))
+        return 0
+
+    lax.fori_loop(0, X, unpack_rim, 0)
+    if M <= X + 6:
+        lax.fori_loop(0, M - X, unpack_far, 0)
+    else:
+        lax.fori_loop(0, 3, unpack_far, 0)
+        lax.fori_loop(0, 3, unpack_low, 0)
 
     def strip_sum(src, q, up, down):
         mine = [src[q, j] for j in range(SITES)]
@@ -170,8 +215,7 @@
 
     m1, m2 = lax.fori_loop(0, min(M, X + 4), first_level, (zero, zero))
 
-    def second_level(i, acc):
-        e = i - 1
+    def second_level(e, acc):
         q, up, down = plane(e), plane(e + 1), plane(e + M - 1)
         mine, sums = strip_sum(s1, q, up, down)
         for j in range(SITES):
@@ -184,10 +228,9 @@
             v2[q, z + 3] = new
             if 0 <= z < Z:
                 three = three + mid * new
-        own = jnp.where((e >= 0) & (e < X), 1.0, 0.0).astype(jnp.float32)
-        return acc + own * three
-
-    m3 = lax.fori_loop(0, X + 2, second_level, zero)
+        return acc + three
+
+    m3 = lax.fori_loop(0, X, second_level, zero)
 
     row = zero
     for n, acc in enumerate((m1, m2, m3)):
@@ -195,21 +238,15 @@
         row = row + jnp.where(lane8 == PROBES * n + probe, summed, 0.0)
     moms[me] = jnp.sum(row, axis=0, keepdims=True)
 
-    def moment_copy(k):
-        to, t = nth(k)
-        out = pltpu.make_async_remote_copy(
-            src_ref=moms.at[me], dst_ref=moms.at[me], send_sem=msend_sem.at[t], recv_sem=mrecv_sem.at[me],
-            device_id=to, device_id_type=MESH)
-        back = pltpu.make_async_remote_copy(
-            src_ref=moms.at[me], dst_ref=moms.at[t], send_sem=msend_sem.at[t], recv_sem=mrecv_sem.at[t],
-            device_id=to, device_id_type=MESH)
-        return out, back
-
-    def send(k, _):
-        moment_copy(k)[0].start()
-        return 0
-
-    lax.fori_loop(1, total, send, 0)
+    each_other(lambda to: pltpu.make_async_remote_copy(
+        src_ref=moms.at[me], dst_ref=moms.at[me], send_sem=msend_sem, recv_sem=mrecv_sem,
+        device_id=to, device_id_type=MESH).start())
+
+    def rim_planes(i, _):
+        second_level(i * (X + 1) - 1, zero)
+        return 0
+
+    lax.fori_loop(0, 2, rim_planes, 0)
 
     def third_level(x, _):
         q, up, down = plane(x), plane(x + 1), plane(x + M - 1)
@@ -224,19 +261,24 @@
 
     lax.fori_loop(0, X, third_level, 0)
 
-    def land(k, _):
-        out, back = moment_copy(k)
-        out.wait_send()
-        back.wait_recv()
-        return 0
-
-    lax.fori_loop(1, total, land, 0)
+    others = moms.at[pl.ds(0, total - 1)]
+    pltpu.make_async_copy(others, others, mrecv_sem).wait()
+    pltpu.make_async_copy(others, others, msend_sem).wait()
     sites = total * X * Z * LANES
     sums = jnp.sum(moms[...], axis=0) * (1.0 / sites)
     first = sums
     second = 2.0 * pltpu.roll(sums, LANES - PROBES, 1) - 1.0
     third = 2.0 * pltpu.roll(sums, LANES - 2 * PROBES, 1) - sums
     mom_ref[...] = jnp.concatenate([first, second, third], axis=0)[:, :PROBES]
+
+
+def write_out(mom_ref, prev_ref, cur_ref, mom_hbm, prev_hbm, cur_hbm, sem):
+    copies = [pltpu.make_async_copy(src, dst, sem.at[n]) for n, (src, dst) in enumerate((
+        (prev_ref, prev_hbm), (cur_ref, cur_hbm), (mom_ref, mom_hbm)))]
+    for copy in copies:
+        copy.start()
+    for copy in copies:
+        copy.wait()
 
 
 def per_device(names, sizes, probe_bits, disorder_levels):
@@ -252,16 +294,20 @@
     vmem = pl.BlockSpec(memory_space=pltpu.VMEM)
     f32, i32 = jnp.float32, jnp.int32
     tile = (PROBES, LANES)
-    moments, previous, current = pl.pallas_call(
+    hbm = pl.BlockSpec(memory_space=pltpu.HBM)
+    out_shape = (
+        jax.ShapeDtypeStruct((3, PROBES), f32),
+        jax.ShapeDtypeStruct((PROBES * X * Z, Y), f32),
+        jax.ShapeDtypeStruct((PROBES * X * Z, Y), f32),
+    )
+    results = pl.pallas_call(
         functools.partial(kernel, names, sizes),
-        out_shape=(
-            jax.ShapeDtypeStruct((3, PROBES), f32),
-            jax.ShapeDtypeStruct((PROBES * X * Z, Y), f32),
-            jax.ShapeDtypeStruct((PROBES * X * Z, Y), f32),
-        ),
-        in_specs=[vmem] * 4,
+        out_shape=out_shape,
+        in_specs=[hbm] * 4,
         out_specs=(vmem,) * 3,
         scratch_shapes=[
+            pltpu.VMEM((X, W, Y), i32),
+            pltpu.VMEM((X, W, Y), i32),
             pltpu.VMEM((2, M, W + 2, 1, LANES), i32),
             pltpu.VMEM((nbx, 3, 3, 2 * X, LANES), i32),
             pltpu.VMEM((nbx, 2 * X, LANES), i32),
@@ -274,14 +320,23 @@
             pltpu.VMEM((M, SITES) + tile, f32),
             pltpu.VMEM((M, SITES) + tile, f32),
             pltpu.VMEM((total, 1, LANES), f32),
+            pltpu.SemaphoreType.DMA((4,)),
             pltpu.SemaphoreType.DMA((n_copies,)),
             pltpu.SemaphoreType.DMA((n_copies,)),
-            pltpu.SemaphoreType.DMA((total,)),
-            pltpu.SemaphoreType.DMA((total,)),
+            pltpu.SemaphoreType.DMA,
+            pltpu.SemaphoreType.DMA,
         ],
         compiler_params=pltpu.CompilerParams(collective_id=0, has_side_effects=True,
                                              vmem_limit_bytes=40 * 1024 * 1024),
     )(probe_bits, disorder_levels, probe_bits.reshape(rows), disorder_levels.reshape(rows))
+    moments, previous, current = pl.pallas_call(
+        write_out,
+        out_shape=out_shape,
+        in_specs=[vmem] * 3,
+        out_specs=(hbm,) * 3,
+        scratch_shapes=[pltpu.SemaphoreType.DMA((3,))],
+        compiler_params=pltpu.CompilerParams(vmem_limit_bytes=16 * 1024 * 1024),
+    )(*results)
     shape = (PROBES, X, Z, Y)
     return moments, previous.reshape(shape), current.reshape(shape)
 

time: 25.6 us -> 23.3 us (0.910)
  local copies, waits for them, and re-layouts: 3.59 us -> 1.43 us
    unnamed x7 -> x4, local copies, waits for them, and re-layouts: 3.59 us -> 1.43 us
    pallas_call x1 -> x2, Pallas kernels: 21 us -> 20.9 us  [the longest x1 19.9 us: per_device(): pl.pallas_call(functools.partial(kernel, names, sizes), out_shape=out_sha...]
where the time goes in v2:
time: 23.3 us; the launch traced here: 23 us
  Pallas kernels  20.9 us (90%)
  local copies, waits for them, and re-layouts  1.43 us (6%)
  between operations  0.65 us (3%)
    pallas_call x1, Pallas kernels, per_device(): pl.pallas_call(functools.partial(kernel, names, sizes), out_shape=out_sha...  19.9 us
    unnamed x4, local copies, waits for them, and re-layouts  1.43 us
    pallas_call x1, Pallas kernels, per_device(): pl.pallas_call(write_out, out_shape=out_shape, in_specs=[vmem] * 3, out_s...  1 us

profile of v2, /device:TPU:0, one launch (start us, length us, event | category | flops | bytes accessed | tf_op | source)
XLA Modules:
  0.0 23.0 jit_solution(6872550068515235498)
XLA Ops:
  0.6 0.0 copy-start
  0.6 0.7 %copy-done = s32[4,8,128]{2,1,0:T(8,128)S(1)} copy-done((s32[4,8,128]{2,1,0:T(8,128)S(1)}, s32[4,8,128]{2,1,0:T(8,128)}, u32[]{:S(2)}) %copy-start) | copy-done | bytes 16408
  1.3 0.0 copy-start.1
  1.4 0.7 %copy-done.1 = s32[4,8,128]{2,1,0:T(8,128)S(1)} copy-done((s32[4,8,128]{2,1,0:T(8,128)S(1)}, s32[4,8,128]{2,1,0:T(8,128)}, u32[]{:S(2)}) %copy-start.1) | copy-done | bytes 16408
  2.1 19.9 %shard_map.49 = (f32[3,8]{1,0:T(4,128)S(1)}, f32[1024,128]{1,0:T(8,128)S(1)}, f32[1024,128]{1,0:T(8,128)S(1)}) custom-call(s32[4,8,128]{2,1,0:T(8,128)S(1)} %copy-done, s32[4,8,128]{2,1,0:T(8,128)S(1)} %copy-done.1, s32[4,8,1,128]{3,2,1,0:T(1,128)S(1)} %bitcast.4, s32[4,8,1,128]{3,2,1,0:T(1,128)S(1)} %bitcast.5), custom_call_target="tpu_custom_call" | custom-call | tf_op jit(solution)/shard_map/pallas_call | solution.py:303
  22.0 1.0 %shard_map.50 = (f32[3,8]{1,0:T(4,128)}, f32[1024,128]{1,0:T(8,128)}, f32[1024,128]{1,0:T(8,128)}) custom-call(f32[3,8]{1,0:T(4,128)S(1)} %get-tuple-element.9.mom_ref, f32[1024,128]{1,0:T(8,128)S(1)} %get-tuple-element.10.prev_ref, f32[1024,128]{1,0:T(8,128)S(1)} %get-tuple-element.11.cur_ref), custom_call_target="tpu_custom_call" | custom-call | tf_op jit(solution)/shard_map/pallas_call | solution.py:332
Async XLA Ops:
  0.6 0.7 %copy-start = (s32[4,8,128]{2,1,0:T(8,128)S(1)}, s32[4,8,128]{2,1,0:T(8,128)}, u32[]{:S(2)}) copy-start(s32[4,8,128]{2,1,0:T(8,128)} %p_hbm.1) | copy-start | bytes 49156
  1.3 0.7 %copy-start.1 = (s32[4,8,128]{2,1,0:T(8,128)S(1)}, s32[4,8,128]{2,1,0:T(8,128)}, u32[]{:S(2)}) copy-start(s32[4,8,128]{2,1,0:T(8,128)} %d_hbm.1) | copy-start | bytes 49156

commit v3 on v2

--- a/solution.py
+++ b/solution.py
@@ -88,9 +88,9 @@
 
     pl.semaphore_wait(barrier, total - 1)
 
-    xs = (0, 1) if nbx == 2 else (0, 1, -1)
+    xs = (1, 0) if nbx == 2 else (1, -1, 0)
+    near, far = [], []
     slot_of = {0: 0, 1: nbx - 1, -1: 1}
-    copies = []
     for ox in xs:
         for oz in (0, 1, -1):
             for oy in (0, 1, -1):
@@ -106,11 +106,11 @@
                         moves.append((words.at[f, pl.ds(0, X), src_w], words.at[f, pl.ds(s * X, X), dst_w]))
                 moves.append((packs.at[0, 1, 1], packs.at[s, 1 - oz, 1 - oy]))
                 for src, dst in moves:
-                    n = len(copies)
-                    copies.append(pltpu.make_async_remote_copy(
+                    n = len(near) + len(far)
+                    (far if ox else near).append(pltpu.make_async_remote_copy(
                         src_ref=src, dst_ref=dst, send_sem=send_sem.at[n], recv_sem=recv_sem.at[n],
                         device_id=to, device_id_type=MESH))
-    for copy in copies:
+    for copy in far + near:
         copy.start()
     scale = 1.0 / spectral_scale
     e_mul = disorder_width / LEVELS / spectral_scale
@@ -138,10 +138,10 @@
         return 0
 
     lax.fori_loop(0, X, unpack_own, 0)
-    for copy in copies:
+    for copy in near:
         copy.wait()
 
-    for s in range(nbx):
+    def unpack_strips(s):
         def joined(oz):
             return jnp.where(column < 3, packs[s, oz, 0], jnp.where(column < 7, packs[s, oz, 1], packs[s, oz, 2]))
         strip = jnp.where(slot_word == 0, pltpu.roll(joined(0), (-STRIP * W) % LANES, 1), joined(1))
@@ -166,12 +166,8 @@
         unpack(plane(i - 3), range(-3, Z + 3))
         return 0
 
+    unpack_strips(0)
     lax.fori_loop(0, X, unpack_rim, 0)
-    if M <= X + 6:
-        lax.fori_loop(0, M - X, unpack_far, 0)
-    else:
-        lax.fori_loop(0, 3, unpack_far, 0)
-        lax.fori_loop(0, 3, unpack_low, 0)
 
     def strip_sum(src, q, up, down):
         mine = [src[q, j] for j in range(SITES)]
@@ -196,8 +192,7 @@
 
     zero = jnp.zeros((PROBES, LANES), jnp.float32)
 
-    def first_level(i, accs):
-        e = i - 2
+    def first_level(e, accs):
         q, up, down = plane(e), plane(e + 1), plane(e + M - 1)
         mine, sums = strip_sum(s0, q, up, down)
         for j in range(SITES):
@@ -210,10 +205,25 @@
             v1[q, z + 3] = new
             if 0 <= z < Z:
                 one, two = one + mid * new, two + new * new
-        own = jnp.where((e >= 0) & (e < X), 1.0, 0.0).astype(jnp.float32)
-        return accs[0] + own * one, accs[1] + own * two
-
-    m1, m2 = lax.fori_loop(0, min(M, X + 4), first_level, (zero, zero))
+        return accs[0] + one, accs[1] + two
+
+    def first_edge(e):
+        def body(i, accs):
+            return first_level(i * (X - 1) + e * (1 - 2 * i), accs)
+        return body
+
+    accs = lax.fori_loop(1, X - 1, first_level, (zero, zero))
+    for copy in far:
+        copy.wait()
+    for s in range(1, nbx):
+        unpack_strips(s)
+    if M <= X + 6:
+        lax.fori_loop(0, M - X, unpack_far, 0)
+    else:
+        lax.fori_loop(0, 3, unpack_far, 0)
+        lax.fori_loop(0, 3, unpack_low, 0)
+    m1, m2 = lax.fori_loop(0, 2, first_edge(0), accs)
+    lax.fori_loop(0, 2, first_edge(-1), (zero, zero))
 
     def second_level(e, acc):
         q, up, down = plane(e), plane(e + 1), plane(e + M - 1)
@@ -241,6 +251,8 @@
     each_other(lambda to: pltpu.make_async_remote_copy(
         src_ref=moms.at[me], dst_ref=moms.at[me], send_sem=msend_sem, recv_sem=mrecv_sem,
         device_id=to, device_id_type=MESH).start())
+
+    lax.fori_loop(0, min(M, X + 4) - (X + 2), first_edge(-2), (zero, zero))
 
     def rim_planes(i, _):
         second_level(i * (X + 1) - 1, zero)
@@ -328,7 +340,7 @@
         ],
         compiler_params=pltpu.CompilerParams(collective_id=0, has_side_effects=True,
                                              vmem_limit_bytes=40 * 1024 * 1024),
-    )(probe_bits, disorder_levels, probe_bits.reshape(rows), disorder_levels.reshape(rows))
+    )(*[pltpu.with_memory_space_constraint(a, pltpu.HBM) for a in (probe_bits, disorder_levels, probe_bits.reshape(rows), disorder_levels.reshape(rows))])
     moments, previous, current = pl.pallas_call(
         write_out,
         out_shape=out_shape,

time: 23.3 us -> 20.6 us (0.88)
  local copies, waits for them, and re-layouts: 1.43 us -> 0 us
  Pallas kernels: 20.9 us -> 19.7 us
    unnamed x4 -> x0, local copies, waits for them, and re-layouts: 1.43 us -> none
    pallas_call x1, Pallas kernels: 19.9 us -> 18.7 us  [per_device(): pl.pallas_call(functools.partial(kernel, names, sizes), out_shape=out_sha...]
where the time goes in v3:
time: 20.6 us; the launch traced here: 20.3 us
  Pallas kernels  19.7 us (96%)
  between operations  0.64 us (3%)
    pallas_call x1, Pallas kernels, per_device(): pl.pallas_call(functools.partial(kernel, names, sizes), out_shape=out_sha...  18.7 us
    pallas_call x1, Pallas kernels, per_device(): pl.pallas_call(write_out, out_shape=out_shape, in_specs=[vmem] * 3, out_s...  1 us

profile of v3, /device:TPU:0, one launch (start us, length us, event | category | flops | bytes accessed | tf_op | source)
XLA Modules:
  0.0 20.3 jit_solution(12506918898068162675)
XLA Ops:
  0.6 18.7 %shard_map.49 = (f32[3,8]{1,0:T(4,128)S(1)}, f32[1024,128]{1,0:T(8,128)S(1)}, f32[1024,128]{1,0:T(8,128)S(1)}) custom-call(s32[4,8,128]{2,1,0:T(8,128)} %p_hbm.1, s32[4,8,128]{2,1,0:T(8,128)} %d_hbm.1, s32[4,8,1,128]{3,2,1,0:T(1,128)} %bitcast.4, s32[4,8,1,128]{3,2,1,0:T(1,128)} %bitcast.5), custom_call_target="tpu_custom_call" | custom-call | tf_op jit(solution)/shard_map/pallas_call | solution.py:315
  19.3 1.0 %shard_map.50 = (f32[3,8]{1,0:T(4,128)}, f32[1024,128]{1,0:T(8,128)}, f32[1024,128]{1,0:T(8,128)}) custom-call(f32[3,8]{1,0:T(4,128)S(1)} %get-tuple-element.9.mom_ref, f32[1024,128]{1,0:T(8,128)S(1)} %get-tuple-element.10.prev_ref, f32[1024,128]{1,0:T(8,128)S(1)} %get-tuple-element.11.cur_ref), custom_call_target="tpu_custom_call" | custom-call | tf_op jit(solution)/shard_map/pallas_call | solution.py:344

commit v4 on v3

--- a/solution.py
+++ b/solution.py
@@ -20,7 +20,7 @@
 
 def kernel(names, sizes, p_hbm, d_hbm, prow_hbm, drow_hbm, mom_ref, prev_ref, cur_ref,
            p_ref, d_ref, words, packs, strips, v0, v1, v2, en, s0, s1, s2, se, moms,
-           load_sem, send_sem, recv_sem, msend_sem, mrecv_sem):
+           load_sem, send_sem, recv_sem, msend_sem, mrecv_sem, ready_sem):
     X, W, _ = p_ref.shape
     Z = SITES * W
     nbx = packs.shape[0]
@@ -68,8 +68,18 @@
                 return 0
             lax.fori_loop(1, gz, step, 0)
 
+    def each_near(act):
+        for x in around_x if nbx == 2 else (around_x[0], around_x[1], around_x[-1]):
+            for y in (around_y[0], around_y[1], around_y[-1]):
+                for z in (iz, lax.rem(iz + 1, gz), lax.rem(iz + gz - 1, gz)):
+                    if not (x is ix and y is iy and z is iz):
+                        act(device(x, y, z))
+
+    two_steps = max(gx, gy, gz) <= 5
+    n_near = 9 * nbx - 1
     barrier = pltpu.get_barrier_semaphore()
-    each_other(lambda to: pl.semaphore_signal(barrier, inc=1, device_id=to, device_id_type=MESH))
+    (each_near if two_steps else each_other)(
+        lambda to: pl.semaphore_signal(barrier, inc=1, device_id=to, device_id_type=MESH))
 
     lane = lax.broadcasted_iota(jnp.int32, (2 * X, LANES), 1)
     slot_word = (lane * 10923) >> 17
@@ -86,7 +96,7 @@
         pack = jnp.where(slot_word == w + 1, jnp.where(column < 5, first, second), pack)
     packs[0, 1, 1] = pack
 
-    pl.semaphore_wait(barrier, total - 1)
+    pl.semaphore_wait(barrier, n_near if two_steps else total - 1)
 
     xs = (1, 0) if nbx == 2 else (1, -1, 0)
     near, far = [], []
@@ -112,6 +122,8 @@
                         device_id=to, device_id_type=MESH))
     for copy in far + near:
         copy.start()
+    if two_steps:
+        each_near(lambda to: pl.semaphore_signal(ready_sem, inc=1, device_id=to, device_id_type=MESH))
     scale = 1.0 / spectral_scale
     e_mul = disorder_width / LEVELS / spectral_scale
     e_add = disorder_width * (0.5 / LEVELS - 0.5) / spectral_scale
@@ -248,6 +260,8 @@
         row = row + jnp.where(lane8 == PROBES * n + probe, summed, 0.0)
     moms[me] = jnp.sum(row, axis=0, keepdims=True)
 
+    if two_steps:
+        pl.semaphore_wait(ready_sem, n_near)
     each_other(lambda to: pltpu.make_async_remote_copy(
         src_ref=moms.at[me], dst_ref=moms.at[me], send_sem=msend_sem, recv_sem=mrecv_sem,
         device_id=to, device_id_type=MESH).start())
@@ -337,6 +351,7 @@
             pltpu.SemaphoreType.DMA((n_copies,)),
             pltpu.SemaphoreType.DMA,
             pltpu.SemaphoreType.DMA,
+            pltpu.SemaphoreType.REGULAR,
         ],
         compiler_params=pltpu.CompilerParams(collective_id=0, has_side_effects=True,
                                              vmem_limit_bytes=40 * 1024 * 1024),

time: 20.6 us -> 21.1 us (1.024)
  Pallas kernels: 19.7 us -> 20.2 us
    pallas_call x1, Pallas kernels: 18.7 us -> 19.2 us  [per_device(): pl.pallas_call(functools.partial(kernel, names, sizes), out_shape=out_sha...]
where the time goes in v4:
time: 21.1 us; the launch traced here: 20.9 us
  Pallas kernels  20.2 us (96%)
  between operations  0.64 us (3%)
    pallas_call x1, Pallas kernels, per_device(): pl.pallas_call(functools.partial(kernel, names, sizes), out_shape=out_sha...  19.2 us
    pallas_call x1, Pallas kernels, per_device(): pl.pallas_call(write_out, out_shape=out_shape, in_specs=[vmem] * 3, out_s...  1 us

profile of v4, /device:TPU:0, one launch (start us, length us, event | category | flops | bytes accessed | tf_op | source)
XLA Modules:
  0.0 20.9 jit_solution(14664340397800529026)
XLA Ops:
  0.6 19.2 %shard_map.49 = (f32[3,8]{1,0:T(4,128)S(1)}, f32[1024,128]{1,0:T(8,128)S(1)}, f32[1024,128]{1,0:T(8,128)S(1)}) custom-call(s32[4,8,128]{2,1,0:T(8,128)} %p_hbm.1, s32[4,8,128]{2,1,0:T(8,128)} %d_hbm.1, s32[4,8,1,128]{3,2,1,0:T(1,128)} %bitcast.4, s32[4,8,1,128]{3,2,1,0:T(1,128)} %bitcast.5), custom_call_target="tpu_custom_call" | custom-call | tf_op jit(solution)/shard_map/pallas_call | solution.py:329
  19.9 1.0 %shard_map.50 = (f32[3,8]{1,0:T(4,128)}, f32[1024,128]{1,0:T(8,128)}, f32[1024,128]{1,0:T(8,128)}) custom-call(f32[3,8]{1,0:T(4,128)S(1)} %get-tuple-element.9.mom_ref, f32[1024,128]{1,0:T(8,128)S(1)} %get-tuple-element.10.prev_ref, f32[1024,128]{1,0:T(8,128)S(1)} %get-tuple-element.11.cur_ref), custom_call_target="tpu_custom_call" | custom-call | tf_op jit(solution)/shard_map/pallas_call | solution.py:359
